TPU v7x, 32 devices: a whole 2x2x4 slice. The times are simulated.
32 devices in a mesh: head: 4 (over z), ctx: 8 (over y, x, core).
Axes of the slice: x: 2, y: 2, z: 4, core: 2. Of those that a mesh axis runs over, the one named last changes fastest.
Arguments:
- queries: bfloat16 [8192, 4, 128], P('ctx', 'head'), may hold values from -120 to 120
- keys: bfloat16 [8192, 4, 128], P('ctx', 'head'), may hold values from -6 to 6
- values: bfloat16 [8192, 4, 128], P('ctx', 'head'), may hold values from -6 to 6
- house: bfloat16 [8192, 4, 128], P('ctx', 'head'), may hold values from -6 to 6
- rates: float32 [4, 8192], P('head', 'ctx'), may hold values from 0.0002 to 1.9, as said below
- out_weight: bfloat16 [512, 8192], P('head'), may hold values from -0.375 to 0.375
Outputs:
- attended: bfloat16 [8192, 4, 128], P('ctx', 'head')
- projected: bfloat16 [8192, 8192], P('ctx', 'head')
Inputs may be any that keep to these rules, and one draw needn't show every extreme that they name: `rates`: strictly positive and below 2, so every transition is a contraction.
All inputs are finite; a program needn't handle non-finite values.
Results may differ from a plain program's by a relative error of at most 0.015.
Values may be sent and summed in bfloat16 or wider, within the bound.
A program may use at most 64 MiB of HBM per device.

v0:
```python
import functools

import jax
import jax.numpy as jnp
from jax import lax
from jax.experimental import pallas as pl
from jax.experimental.pallas import tpu as pltpu
from jax.sharding import PartitionSpec as P

EPSILON = 1e-06
NEGATIVE = -1e30
MESH = pl.DeviceIdType.MESH
F32 = jnp.float32
BF16 = jnp.bfloat16


def mm(a, b):
    return jnp.dot(a, b, preferred_element_type=F32)


def split(x):
    high = x.astype(BF16)
    return high, (x - high.astype(F32)).astype(BF16)


def dot3(a, b):
    (ah, al), (bh, bl) = split(a), split(b)
    if a.shape[1] <= 128:
        return mm(jnp.concatenate([ah, al], 1), jnp.concatenate([bh, bh], 0)) + mm(ah, bl)
    return mm(ah, bh) + mm(al, bh) + mm(ah, bl)


def kernel(
    n_ctx, n_head, block,
    q_ref, k_ref, v_ref, h_ref, rates_ref, w_ref,
    att_ref, flat_ref, cols_ref,
    kall, vall, tall, ksend, tsend, nmat, inv, moved, mov, acc, peak, total,
    v_ssem, v_rsem, k_ssem, k_rsem, t_ssem, t_rsem, w_ssem, w_rsem, a_ssem, a_rsem, loc_sem,
):
    me = lax.axis_index("ctx")
    head = lax.axis_index("head")
    rows, feat = q_ref.shape
    blocks = rows // block
    width = cols_ref.shape[1]
    scale = feat ** (-0.5)

    barrier = pltpu.get_barrier_semaphore()
    for step in range(1, n_ctx):
        pl.semaphore_signal(barrier, inc=1, device_id={"ctx": lax.rem(me + step, n_ctx)}, device_id_type=MESH)
    for step in range(1, n_head):
        pl.semaphore_signal(barrier, inc=1, device_id={"head": lax.rem(head + step, n_head)}, device_id_type=MESH)
    pl.semaphore_wait(barrier, n_ctx + n_head - 2)

    def v_copy(owner, peer):
        return pltpu.make_async_remote_copy(
            src_ref=v_ref, dst_ref=vall.at[owner], send_sem=v_ssem.at[peer], recv_sem=v_rsem.at[owner],
            device_id={"ctx": peer}, device_id_type=MESH)

    def k_copy(owner, peer):
        return pltpu.make_async_remote_copy(
            src_ref=ksend, dst_ref=kall.at[owner], send_sem=k_ssem.at[peer], recv_sem=k_rsem.at[owner],
            device_id={"ctx": peer}, device_id_type=MESH)

    def t_copy(owner, peer):
        return pltpu.make_async_remote_copy(
            src_ref=tsend, dst_ref=tall.at[owner], send_sem=t_ssem.at[peer], recv_sem=t_rsem.at[owner],
            device_id={"ctx": peer}, device_id_type=MESH)

    def w_copy(owner, peer):
        return pltpu.make_async_remote_copy(
            src_ref=w_ref.at[:, pl.ds(pl.multiple_of(peer * width, 128), width)],
            dst_ref=cols_ref.at[pl.ds(pl.multiple_of(owner * feat, 128), feat), :],
            send_sem=w_ssem.at[peer], recv_sem=w_rsem.at[owner],
            device_id={"head": peer}, device_id_type=MESH)

    def a_copy(owner, peer):
        return pltpu.make_async_remote_copy(
            src_ref=att_ref, dst_ref=flat_ref.at[:, pl.ds(pl.multiple_of(owner * feat, 128), feat)],
            send_sem=a_ssem.at[peer], recv_sem=a_rsem.at[owner],
            device_id={"head": peer}, device_id_type=MESH)

    def later(action):
        def go(peer, carry):
            action(peer)
            return carry
        lax.fori_loop(me + 1, n_ctx, go, 0)

    later(lambda peer: v_copy(me, peer).start())
    for step in range(1, n_head):
        w_copy(head, lax.rem(head + step, n_head)).start()
    w_own = pltpu.make_async_copy(
        w_ref.at[:, pl.ds(pl.multiple_of(head * width, 128), width)],
        cols_ref.at[pl.ds(pl.multiple_of(head * feat, 128), feat), :], loc_sem.at[0])
    w_own.start()

    ri = lax.broadcasted_iota(jnp.int32, (block, block), 0)
    ci = lax.broadcasted_iota(jnp.int32, (block, block), 1)
    eye = ri == ci
    strict = ri > ci
    nt = (((1,), (1,)), ((), ()))

    scales = []
    for b in range(blocks):
        part = slice(b * block, (b + 1) * block)
        hb = h_ref[part, :]
        gram = lax.dot_general(hb, hb, nt, preferred_element_type=F32)
        diag = jnp.where(eye, gram, 0.0)
        r_col = lax.rsqrt(jnp.sum(diag, axis=1, keepdims=True) + EPSILON)
        r_row = lax.rsqrt(jnp.sum(diag, axis=0, keepdims=True) + EPSILON)
        beta_row = rates_ref[:, part]
        beta_col = jnp.sum(jnp.where(eye, beta_row, 0.0), axis=1, keepdims=True)
        lower = jnp.where(strict, gram * (beta_col * r_col) * r_row, 0.0)
        nmat[b] = lower
        first = jnp.logical_and((ri >> 1) == (ci >> 1), strict)
        inv[b] = jnp.where(eye, 1.0, 0.0) - jnp.where(first, lower, 0.0)
        scales.append((r_col, r_row * beta_row))

    def level(depth, carry):
        near = jnp.logical_and((ri >> (depth + 1)) == (ci >> (depth + 1)), (ri >> depth) != (ci >> depth))
        xs = [inv[b] for b in range(blocks)]
        parts = [split(x) for x in xs]
        ys = []
        for b in range(blocks):
            (mh, ml), (xh, xl) = split(jnp.where(near, nmat[b], 0.0)), parts[b]
            ys.append(mm(mh, xh) + mm(ml, xh) + mm(mh, xl))
        for b in range(blocks):
            (yh, yl), (xh, xl) = split(ys[b]), parts[b]
            inv[b] = xs[b] - (mm(xh, yh) + mm(xl, yh) + mm(xh, yl))
        return carry

    lax.fori_loop(1, block.bit_length() - 1, level, 0)

    fr = lax.broadcasted_iota(jnp.int32, (feat, feat), 0)
    fc = lax.broadcasted_iota(jnp.int32, (feat, feat), 1)
    unit = jnp.where(fr == fc, 1.0, 0.0).astype(F32)
    rights, passages, finals = [], [], []
    for b in range(blocks):
        part = slice(b * block, (b + 1) * block)
        hb, kb = h_ref[part, :], k_ref[part, :]
        r_col, rb_row = scales[b]
        th, tl = split(inv[b] * r_col * rb_row)
        wk = lax.dot_general(hb, kb, nt, preferred_element_type=F32)
        wh, wl = split(jnp.where(strict, wk, 0.0))
        rk = mm(th, wh) + mm(tl, wh) + mm(th, wl)
        rh = mm(th, hb) + mm(tl, hb)
        hbt = hb.astype(F32).T.astype(BF16)
        rkh, rkl = split(rk)
        rhh, rhl = split(rh)
        finals.append(kb.astype(F32).T - (mm(hbt, rkh) + mm(hbt, rkl)))
        passages.append(unit - (mm(hbt, rhh) + mm(hbt, rhl)))
        rights.append((rkh, rkl, rhh, rhl))

    prefixes = [None]
    now = finals[0]
    prefix = passages[0]
    for b in range(1, blocks):
        moved[b - 1, :, : b * block] = now
        prefixes.append(prefix)
        now = jnp.concatenate([dot3(passages[b], now), finals[b]], 1)
        prefix = dot3(passages[b], prefix)
    ksend[...] = now.astype(BF16)
    tsend[...] = prefix
    def both(peer):
        t_copy(me, peer).start()
        k_copy(me, peer).start()
    later(both)

    for b in range(blocks):
        part = slice(b * block, (b + 1) * block)
        hb, kb, qb = h_ref[part, :], k_ref[part, :], q_ref[part, :]
        rkh, rkl, rhh, rhl = rights[b]
        qw = lax.dot_general(qb, hb, nt, preferred_element_type=F32)
        qwh, qwl = split(jnp.where(ri >= ci, qw, 0.0))
        qk = lax.dot_general(qb, kb, nt, preferred_element_type=F32)
        inside = (qk - (mm(qwh, rkh) + mm(qwl, rkh) + mm(qwh, rkl))) * scale
        scores = jnp.where(ri >= ci, inside, NEGATIVE)
        start = (qb.astype(F32) - (mm(qwh, rhh) + mm(qwl, rhh) + mm(qwh, rhl))) * scale
        if b:
            scores = jnp.concatenate([dot3(start, moved[b - 1, :, : b * block]), scores], 1)
            mov[part, :] = dot3(start, prefixes[b])
        else:
            mov[part, :] = start
        top = jnp.max(scores, axis=1, keepdims=True)
        weight = jnp.exp(scores - top)
        peak[part, :] = top
        total[part, :] = jnp.sum(weight, axis=1, keepdims=True)
        acc[part, :] = mm(weight.astype(BF16), v_ref[: (b + 1) * block, :])

    def visit(offset, carry):
        source = me - 1 - offset
        t_copy(source, me).wait_recv()
        k_copy(source, me).wait_recv()
        v_copy(source, me).wait_recv()
        keys = kall[source]
        keys2 = jnp.concatenate([keys, keys], 0)
        vals = vall[source]
        th, tl = split(tall[source])
        th2 = jnp.concatenate([th, th], 0)

        def tile(t, inner):
            part = pl.ds(pl.multiple_of(t * block, block), block)
            qh, ql = split(mov[part, :])
            both = jnp.concatenate([qh, ql], 1)
            scores = mm(both, keys2)
            old = peak[part, :]
            top = jnp.maximum(old, jnp.max(scores, axis=1, keepdims=True))
            weight = jnp.exp(scores - top)
            shrink = jnp.exp(old - top)
            peak[part, :] = top
            total[part, :] = total[part, :] * shrink + jnp.sum(weight, axis=1, keepdims=True)
            acc[part, :] = acc[part, :] * shrink + mm(weight.astype(BF16), vals)
            mov[part, :] = mm(both, th2) + mm(qh, tl)
            return inner

        lax.fori_loop(0, blocks, tile, 0)
        return carry

    lax.fori_loop(0, me, visit, 0)

    att_ref[...] = (acc[...] / total[...]).astype(BF16)
    for step in range(1, n_head):
        a_copy(head, lax.rem(head + step, n_head)).start()
    a_own = pltpu.make_async_copy(
        att_ref, flat_ref.at[:, pl.ds(pl.multiple_of(head * feat, 128), feat)], loc_sem.at[1])
    a_own.start()
    w_own.wait()
    def sent(peer):
        v_copy(me, peer).wait_send()
        t_copy(me, peer).wait_send()
        k_copy(me, peer).wait_send()
    later(sent)
    for step in range(1, n_head):
        other = lax.rem(head + step, n_head)
        w_copy(head, other).wait_send()
        w_copy(other, head).wait_recv()
        a_copy(head, other).wait_send()
        a_copy(other, head).wait_recv()
    a_own.wait()


def solution(mesh):
    n_ctx, n_head = mesh.shape["ctx"], mesh.shape["head"]

    def body(queries, keys, values, house, rates, out_weight):
        rows, _, feat = queries.shape
        block = min(256, rows)
        blocks = rows // block
        width = out_weight.shape[1] // n_head
        vmem = pl.BlockSpec(memory_space=pltpu.VMEM)
        hbm = pl.BlockSpec(memory_space=pl.ANY)
        dma = pltpu.SemaphoreType.DMA
        attended, flat, columns = pl.pallas_call(
            functools.partial(kernel, n_ctx, n_head, block),
            out_shape=(
                jax.ShapeDtypeStruct((rows, feat), BF16),
                jax.ShapeDtypeStruct((rows, n_head * feat), BF16),
                jax.ShapeDtypeStruct((n_head * feat, width), BF16),
            ),
            in_specs=[vmem] * 5 + [hbm],
            out_specs=(vmem, hbm, hbm),
            scratch_shapes=[
                pltpu.VMEM((n_ctx, feat, rows), BF16),
                pltpu.VMEM((n_ctx, rows, feat), BF16),
                pltpu.VMEM((n_ctx, feat, feat), F32),
                pltpu.VMEM((feat, rows), BF16),
                pltpu.VMEM((feat, feat), F32),
                pltpu.VMEM((blocks, block, block), F32),
                pltpu.VMEM((blocks, block, block), F32),
                pltpu.VMEM((max(blocks - 1, 1), feat, rows), F32),
                pltpu.VMEM((rows, feat), F32),
                pltpu.VMEM((rows, feat), F32),
                pltpu.VMEM((rows, 1), F32),
                pltpu.VMEM((rows, 1), F32),
                dma((n_ctx,)), dma((n_ctx,)), dma((n_ctx,)), dma((n_ctx,)), dma((n_ctx,)), dma((n_ctx,)),
                dma((n_head,)), dma((n_head,)), dma((n_head,)), dma((n_head,)), dma((2,)),
            ],
            compiler_params=pltpu.CompilerParams(
                collective_id=0, has_side_effects=True, vmem_limit_bytes=60 * 1024 * 1024),
            name="path_attention",
        )(queries.reshape(rows, feat), keys.reshape(rows, feat), values.reshape(rows, feat),
          house.reshape(rows, feat), rates, out_weight)
        projected = jnp.dot(flat, columns, preferred_element_type=F32)
        return attended.reshape(rows, 1, feat), projected.astype(BF16)

    in_specs = (
        P("ctx", "head", None),
        P("ctx", "head", None),
        P("ctx", "head", None),
        P("ctx", "head", None),
        P("head", "ctx"),
        P("head", None),
    )
    out_specs = (P("ctx", "head", None), P("ctx", "head"))
    return jax.shard_map(body, mesh=mesh, in_specs=in_specs, out_specs=out_specs, check_vma=False)
```

profile of v0, /device:TPU:13, one launch (start us, length us, event | category | flops | bytes accessed | tf_op | source)
XLA Modules:
  0.0 90.9 jit_solution(7129240809279476410)
XLA Ops:
  0.6 83.2 %path_attention.1 = (bf16[1024,128]{1,0:T(8,128)(2,1)}, bf16[1024,512]{1,0:T(8,128)(2,1)}, bf16[512,2048]{1,0:T(8,128)(2,1)}) custom-call(bf16[1024,128]{1,0:T(8,128)(2,1)} %bitcast.7, bf16[1024,128]{1,0:T(8,128)(2,1)} %bitcast.8, bf16[1024,128]{1,0:T(8,128)(2,1)} %bitcast.9, bf16[1024,128]{1,0:T(8,128)(2,1)} %bitcast.10, f32[1,1024]{1,0:T(1,128)} %rates_ref.1, ...), custom_call_target="tpu_custom_call" | custom-call | tf_op jit(solution)/shard_map/path_attention/pallas_call | solution.py:252
  83.8 0.0 copy-start
  83.8 6.3 %convolution_convert_fusion = bf16[1024,2048]{1,0:T(8,128)(2,1)} fusion(bf16[1024,512]{1,0:T(8,128)(2,1)} %get-tuple-element.6, bf16[512,2048]{1,0:T(8,128)(2,1)} %get-tuple-element.7), kind=kOutput, calls=%fused_computation | convolution fusion | flops 2149580800 | bytes 7340032 | tf_op jit(solution)/shard_map/dot_general | solution.py:282
  90.1 0.0 copy-done
  90.2 0.7 copy.9
Async XLA Ops:
  83.8 6.3 %copy-start = (bf16[1024,128]{1,0:T(8,128)(2,1)S(1)}, bf16[1024,128]{1,0:T(8,128)(2,1)}, u32[]{:S(2)}) copy-start(bf16[1024,128]{1,0:T(8,128)(2,1)} %get-tuple-element.5) | copy-start | bytes 786436
where the time goes:
time: 91 us; the launch traced here: 90.9 us
  Pallas kernels  83.2 us (91%)
  matrix products  6.31 us (7%)
    pallas_call x1, Pallas kernels, body(): pl.pallas_call(functools.partial(kernel, n_ctx, n_head, block), out_shape...  83.2 us
    dot_general x1, matrix products, body(): projected = jnp.dot(flat, columns, preferred_element_type=F32)  6.31 us

commit v1 on v0

v1 whole, which is shorter than its diff:
```python
import functools

import jax
import jax.numpy as jnp
from jax import lax
from jax.experimental import pallas as pl
from jax.experimental.pallas import tpu as pltpu
from jax.sharding import PartitionSpec as P

EPSILON = 1e-06
NEGATIVE = -1e30
MESH = pl.DeviceIdType.MESH
F32 = jnp.float32
BF16 = jnp.bfloat16
NT = (((1,), (1,)), ((), ()))


def mm(a, b):
    return jnp.dot(a, b, preferred_element_type=F32)


def split(x):
    high = x.astype(BF16)
    return high, (x - high.astype(F32)).astype(BF16)


def dot3(a, b):
    (ah, al), (bh, bl) = split(a), split(b)
    if a.shape[1] <= 128:
        return mm(jnp.concatenate([ah, al], 1), jnp.concatenate([bh, bh], 0)) + mm(ah, bl)
    return mm(ah, bh) + mm(al, bh) + mm(ah, bl)


def kernel(
    n_ctx, n_head, block, halves,
    q_ref, k_ref, v_ref, h_ref, rates_ref, w_ref,
    flat_ref, cols_ref,
    kall, vall, wbuf, att, nmat, inv, moved, mov, acc, peak, total,
    v_ssem, v_fsem, v_rsem, k_ssem, k_fsem, k_rsem,
    w_ssem, w_rsem, wf_ssem, wf_rsem, a_ssem, a_rsem, a_fsem, own_sem, out_sem,
):
    me = lax.axis_index("ctx")
    head = lax.axis_index("head")
    rows, feat = q_ref.shape
    blocks = rows // block
    width = wbuf.shape[1]
    half_width = width // 2
    scale = feat ** (-0.5)
    odd = lax.rem(me, 2)
    partner = me + 1 - 2 * odd
    later_pairs = (n_ctx - 1 - me) // 2
    earlier_pairs = me // 2
    span = rows // halves

    barrier = pltpu.get_barrier_semaphore()
    for step in range(1, n_ctx):
        pl.semaphore_signal(barrier, inc=1, device_id={"ctx": lax.rem(me + step, n_ctx)}, device_id_type=MESH)
    for step in range(1, n_head):
        pl.semaphore_signal(barrier, inc=1, device_id={"head": lax.rem(head + step, n_head)}, device_id_type=MESH)
    pl.semaphore_wait(barrier, n_ctx + n_head - 2)

    def slab(buf, owner, send, recv, peer):
        return pltpu.make_async_remote_copy(
            src_ref=buf.at[owner], dst_ref=buf.at[owner], send_sem=send, recv_sem=recv.at[owner],
            device_id={"ctx": peer}, device_id_type=MESH)

    def v_copy(owner, peer):
        return slab(vall, owner, v_ssem.at[peer], v_rsem, peer)

    def k_copy(owner, peer):
        return slab(kall, owner, k_ssem.at[peer], k_rsem, peer)

    def v_forward(owner):
        return slab(vall, owner, v_fsem.at[owner], v_rsem, partner)

    def k_forward(owner):
        return slab(kall, owner, k_fsem.at[owner], k_rsem, partner)

    def to_later(copy, action):
        def go(i, carry):
            action(copy(me, me + 2 * (later_pairs - i)))
            return carry
        lax.fori_loop(0, later_pairs, go, 0)

        @pl.when(odd == 0)
        def _():
            action(copy(me, me + 1))

    def half_cols(base, which):
        return pl.ds(pl.multiple_of(base + which * half_width, 128), half_width)

    def w_copy(owner, peer):
        return pltpu.make_async_remote_copy(
            src_ref=w_ref.at[:, half_cols(peer * width, odd)],
            dst_ref=wbuf.at[pl.ds(pl.multiple_of(owner * feat, 128), feat), half_cols(0, odd)],
            send_sem=w_ssem.at[peer], recv_sem=w_rsem.at[owner],
            device_id={"head": peer}, device_id_type=MESH)

    def w_swap(owner, which):
        part = wbuf.at[pl.ds(pl.multiple_of(owner * feat, 128), feat), half_cols(0, which)]
        return pltpu.make_async_remote_copy(
            src_ref=part, dst_ref=part, send_sem=wf_ssem.at[owner], recv_sem=wf_rsem.at[owner],
            device_id={"ctx": partner}, device_id_type=MESH)

    def a_rows(part):
        return pl.ds(part * span, span)

    def a_cols(owner):
        return pl.ds(pl.multiple_of(owner * feat, 128), feat)

    def a_copy(owner, peer, part):
        return pltpu.make_async_remote_copy(
            src_ref=att.at[a_rows(part), :], dst_ref=flat_ref.at[a_rows(part), a_cols(owner)],
            send_sem=a_ssem.at[part, peer], recv_sem=a_rsem.at[part, owner],
            device_id={"head": peer}, device_id_type=MESH)

    def a_relay(owner, peer, part):
        piece = flat_ref.at[a_rows(part), a_cols(owner)]
        return pltpu.make_async_remote_copy(
            src_ref=piece, dst_ref=piece,
            send_sem=a_fsem.at[part, owner], recv_sem=a_rsem.at[part, owner],
            device_id={"head": peer}, device_id_type=MESH)

    for step in range(1, n_head):
        w_copy(head, lax.rem(head + step, n_head)).start()
    w_own = pltpu.make_async_copy(
        w_ref.at[:, pl.ds(pl.multiple_of(head * width, 128), width)],
        wbuf.at[pl.ds(pl.multiple_of(head * feat, 128), feat), :], own_sem.at[0])
    w_own.start()

    vall[me] = v_ref[...].T

    ri = lax.broadcasted_iota(jnp.int32, (block, block), 0)
    ci = lax.broadcasted_iota(jnp.int32, (block, block), 1)
    eye = ri == ci
    strict = ri > ci

    scales = []
    for b in range(blocks):
        part = slice(b * block, (b + 1) * block)
        hb = h_ref[part, :]
        gram = lax.dot_general(hb, hb, NT, preferred_element_type=F32)
        diag = jnp.where(eye, gram, 0.0)
        r_col = lax.rsqrt(jnp.sum(diag, axis=1, keepdims=True) + EPSILON)
        r_row = lax.rsqrt(jnp.sum(diag, axis=0, keepdims=True) + EPSILON)
        beta_row = rates_ref[:, part]
        beta_col = jnp.sum(jnp.where(eye, beta_row, 0.0), axis=1, keepdims=True)
        lower = jnp.where(strict, gram * (beta_col * r_col) * r_row, 0.0)
        nmat[b] = lower
        first = jnp.logical_and((ri >> 1) == (ci >> 1), strict)
        inv[b] = jnp.where(eye, 1.0, 0.0) - jnp.where(first, lower, 0.0)
        scales.append((r_col, r_row * beta_row))

    to_later(v_copy, lambda copy: copy.start())

    def level(depth, carry):
        near = jnp.logical_and((ri >> (depth + 1)) == (ci >> (depth + 1)), (ri >> depth) != (ci >> depth))
        xs = [inv[b] for b in range(blocks)]
        parts = [split(x) for x in xs]
        ys = []
        for b in range(blocks):
            (mh, ml), (xh, xl) = split(jnp.where(near, nmat[b], 0.0)), parts[b]
            ys.append(mm(mh, xh) + mm(ml, xh) + mm(mh, xl))
        for b in range(blocks):
            (yh, yl), (xh, xl) = split(ys[b]), parts[b]
            inv[b] = xs[b] - (mm(xh, yh) + mm(xl, yh) + mm(xh, yl))
        return carry

    lax.fori_loop(1, block.bit_length() - 1, level, 0)

    fr = lax.broadcasted_iota(jnp.int32, (feat, feat), 0)
    fc = lax.broadcasted_iota(jnp.int32, (feat, feat), 1)
    unit = jnp.where(fr == fc, 1.0, 0.0).astype(F32)
    rights, passages, finals = [], [], []
    for b in range(blocks):
        part = slice(b * block, (b + 1) * block)
        hb, kb = h_ref[part, :], k_ref[part, :]
        r_col, rb_row = scales[b]
        th, tl = split(inv[b] * r_col * rb_row)
        wk = lax.dot_general(hb, kb, NT, preferred_element_type=F32)
        wh, wl = split(jnp.where(strict, wk, 0.0))
        rk = mm(th, wh) + mm(tl, wh) + mm(th, wl)
        rh = mm(th, hb) + mm(tl, hb)
        hbt = hb.astype(F32).T.astype(BF16)
        rkh, rkl = split(rk)
        rhh, rhl = split(rh)
        finals.append(kb.astype(F32).T - (mm(hbt, rkh) + mm(hbt, rkl)))
        passages.append(unit - (mm(hbt, rhh) + mm(hbt, rhl)))
        rights.append((rkh, rkl, rhh, rhl))

    prefixes = [None]
    now = finals[0]
    prefix = passages[0]
    for b in range(1, blocks):
        moved[b - 1, :, : b * block] = now
        prefixes.append(prefix)
        now = jnp.concatenate([dot3(passages[b], now), finals[b]], 1)
        prefix = dot3(passages[b], prefix)
    kall[me, :rows, :] = now.T.astype(BF16)
    kall[me, rows:, :] = prefix.T.astype(BF16)
    to_later(k_copy, lambda copy: copy.start())

    def pass_values(i, carry):
        source = me - 2 - 2 * i
        v_copy(source, me).wait_recv()
        v_forward(source).start()
        return carry
    lax.fori_loop(0, earlier_pairs, pass_values, 0)

    for b in range(blocks):
        part = slice(b * block, (b + 1) * block)
        hb, kb, qb = h_ref[part, :], k_ref[part, :], q_ref[part, :]
        rkh, rkl, rhh, rhl = rights[b]
        qw = lax.dot_general(qb, hb, NT, preferred_element_type=F32)
        qwh, qwl = split(jnp.where(ri >= ci, qw, 0.0))
        qk = lax.dot_general(qb, kb, NT, preferred_element_type=F32)
        inside = (qk - (mm(qwh, rkh) + mm(qwl, rkh) + mm(qwh, rkl))) * scale
        scores = jnp.where(ri >= ci, inside, NEGATIVE)
        start = (qb.astype(F32) - (mm(qwh, rhh) + mm(qwl, rhh) + mm(qwh, rhl))) * scale
        if b:
            scores = jnp.concatenate([dot3(start, moved[b - 1, :, : b * block]), scores], 1)
            start = dot3(start, prefixes[b])
        mov[:, part] = start.T
        top = jnp.max(scores, axis=1, keepdims=True)
        weight = jnp.exp(scores - top)
        peak[:, part] = jnp.sum(jnp.where(eye, top, 0.0), axis=0, keepdims=True)
        summed = jnp.sum(weight, axis=1, keepdims=True)
        total[:, part] = jnp.sum(jnp.where(eye, summed, 0.0), axis=0, keepdims=True)
        acc[:, part] = mm(weight.astype(BF16), v_ref[: (b + 1) * block, :]).T

    def attend(cols, sources):
        moving = mov[:, cols]
        scores = []
        for source in sources:
            qcat = jnp.concatenate(split(moving), 0)
            keys = kall[source]
            out = mm(jnp.concatenate([keys, keys], 1), qcat)
            scores.append(out[:rows])
            moving = out[rows:]
        mov[:, cols] = moving
        old = peak[:, cols]
        top = old
        for s in scores:
            top = jnp.maximum(top, jnp.max(s, axis=0, keepdims=True))
        shrink = jnp.exp(old - top)
        peak[:, cols] = top
        summed = total[:, cols] * shrink
        gathered = acc[:, cols] * shrink
        for source, s in zip(sources, scores):
            weight = jnp.exp(s - top)
            summed = summed + jnp.sum(weight, axis=0, keepdims=True)
            gathered = gathered + mm(vall[source], weight.astype(BF16))
        total[:, cols] = summed
        acc[:, cols] = gathered

    def relayed(owner, peer):
        if n_head < 3:
            return owner != owner
        return jnp.logical_or(jnp.logical_and(owner == 0, peer == n_head - 1),
                              jnp.logical_and(owner == n_head - 1, peer == 0))

    def direct(part, action):
        for peer in range(n_head):
            @pl.when(jnp.logical_and(head != peer, jnp.logical_not(relayed(head, peer))))
            def _():
                action(a_copy(head, peer, part))

    per_half = span // block
    for part in range(halves):
        @pl.when(odd == 1)
        def _():
            if part == 0:
                k_copy(me - 1, me).wait_recv()
                v_copy(me - 1, me).wait_recv()
            for t in range(per_half):
                attend(pl.ds(part * span + t * block, block), [me - 1])

        def visit(i, carry):
            low = (earlier_pairs - 1 - i) * 2
            if part == 0:
                mine, other = low + odd, low + 1 - odd
                k_copy(mine, me).wait_recv()
                k_forward(mine).start()
                k_copy(other, me).wait_recv()
                v_copy(other, me).wait_recv()
            for t in range(per_half):
                attend(pl.ds(part * span + t * block, block), [low + 1, low])
            return carry

        lax.fori_loop(0, earlier_pairs, visit, 0)
        for t in range(per_half):
            cols = pl.ds(part * span + t * block, block)
            att[cols, :] = (acc[:, cols] / total[:, cols]).T.astype(BF16)
        direct(part, lambda copy: copy.start())
        pltpu.make_async_copy(
            att.at[a_rows(part), :], flat_ref.at[a_rows(part), a_cols(head)], out_sem.at[part]).start()
        if part == 0:
            for step in range(1, n_head):
                other = lax.rem(head + step, n_head)
                w_copy(other, head).wait_recv()
                w_swap(other, odd).start()
            w_own.wait()

    if n_head >= 3:
        for part in range(halves):
            for owner, relay, peer in ((0, n_head - 2, n_head - 1), (n_head - 1, 1, 0)):
                @pl.when(head == relay)
                def _():
                    a_copy(owner, relay, part).wait_recv()
                    a_relay(owner, peer, part).start()

    for step in range(1, n_head):
        w_swap(lax.rem(head + step, n_head), 1 - odd).wait_recv()
    w_out = pltpu.make_async_copy(wbuf, cols_ref, own_sem.at[1])
    w_out.start()

    to_later(v_copy, lambda copy: copy.wait_send())
    to_later(k_copy, lambda copy: copy.wait_send())

    def passed(i, carry):
        source = me - 2 - 2 * i
        v_forward(source).wait_send()
        k_forward(source).wait_send()
        return carry
    lax.fori_loop(0, earlier_pairs, passed, 0)

    for step in range(1, n_head):
        other = lax.rem(head + step, n_head)
        w_copy(head, other).wait_send()
        w_swap(other, odd).wait_send()

    for part in range(halves):
        direct(part, lambda copy: copy.wait_send())
        for owner in range(n_head):
            skip = head != owner
            if n_head >= 3 and owner in (0, n_head - 1):
                relay = n_head - 2 if owner == 0 else 1
                skip = jnp.logical_and(skip, head != relay)

                @pl.when(head == relay)
                def _():
                    a_relay(owner, head, part).wait_send()

            @pl.when(skip)
            def _():
                a_copy(owner, head, part).wait_recv()
        pltpu.make_async_copy(
            att.at[a_rows(part), :], flat_ref.at[a_rows(part), a_cols(head)], out_sem.at[part]).wait()
    w_out.wait()


def project(flat_ref, cols_ref, att_ref, out_ref):
    feat = att_ref.shape[1]

    @pl.when(pl.program_id(0) == 0)
    def _():
        head = lax.axis_index("head")
        att_ref[...] = flat_ref[:, pl.ds(pl.multiple_of(head * feat, 128), feat)]

    out_ref[...] = mm(flat_ref[...], cols_ref[...]).astype(BF16)


def solution(mesh):
    n_ctx, n_head = mesh.shape["ctx"], mesh.shape["head"]

    def body(queries, keys, values, house, rates, out_weight):
        rows, _, feat = queries.shape
        block = min(256, rows)
        blocks = rows // block
        halves = 2 if blocks % 2 == 0 else 1
        width = out_weight.shape[1] // n_head
        vmem = pl.BlockSpec(memory_space=pltpu.VMEM)
        hbm = pl.BlockSpec(memory_space=pl.ANY)
        dma = pltpu.SemaphoreType.DMA
        flat, columns = pl.pallas_call(
            functools.partial(kernel, n_ctx, n_head, block, halves),
            out_shape=(
                jax.ShapeDtypeStruct((rows, n_head * feat), BF16),
                jax.ShapeDtypeStruct((n_head * feat, width), BF16),
            ),
            in_specs=[vmem] * 5 + [hbm],
            out_specs=(hbm, hbm),
            scratch_shapes=[
                pltpu.VMEM((n_ctx, rows + feat, feat), BF16),
                pltpu.VMEM((n_ctx, feat, rows), BF16),
                pltpu.VMEM((n_head * feat, width), BF16),
                pltpu.VMEM((rows, feat), BF16),
                pltpu.VMEM((blocks, block, block), F32),
                pltpu.VMEM((blocks, block, block), F32),
                pltpu.VMEM((max(blocks - 1, 1), feat, rows), F32),
                pltpu.VMEM((feat, rows), F32),
                pltpu.VMEM((feat, rows), F32),
                pltpu.VMEM((1, rows), F32),
                pltpu.VMEM((1, rows), F32),
                dma((n_ctx,)), dma((n_ctx,)), dma((n_ctx,)), dma((n_ctx,)), dma((n_ctx,)), dma((n_ctx,)),
                dma((n_head,)), dma((n_head,)), dma((n_head,)), dma((n_head,)),
                dma((halves, n_head)), dma((halves, n_head)), dma((halves, n_head)), dma((2,)), dma((halves,)),
            ],
            compiler_params=pltpu.CompilerParams(
                collective_id=0, has_side_effects=True, vmem_limit_bytes=60 * 1024 * 1024),
            name="path_attention",
        )(queries.reshape(rows, feat), keys.reshape(rows, feat), values.reshape(rows, feat),
          house.reshape(rows, feat), rates, out_weight)
        tile = min(512, width)
        attended, projected = pl.pallas_call(
            project,
            grid=(width // tile,),
            out_shape=(
                jax.ShapeDtypeStruct((rows, feat), BF16),
                jax.ShapeDtypeStruct((rows, width), BF16),
            ),
            in_specs=[
                pl.BlockSpec((rows, n_head * feat), lambda i: (0, 0)),
                pl.BlockSpec((n_head * feat, tile), lambda i: (0, i)),
            ],
            out_specs=(
                pl.BlockSpec((rows, feat), lambda i: (0, 0)),
                pl.BlockSpec((rows, tile), lambda i: (0, i)),
            ),
            compiler_params=pltpu.CompilerParams(vmem_limit_bytes=40 * 1024 * 1024),
            name="projection",
        )(flat, columns)
        return attended.reshape(rows, 1, feat), projected

    in_specs = (
        P("ctx", "head", None),
        P("ctx", "head", None),
        P("ctx", "head", None),
        P("ctx", "head", None),
        P("head", "ctx"),
        P("head", None),
    )
    out_specs = (P("ctx", "head", None), P("ctx", "head"))
    return jax.shard_map(body, mesh=mesh, in_specs=in_specs, out_specs=out_specs, check_vma=False)
```

time: 91 us -> 68 us (0.75)
  the two profiles are of different devices: /device:TPU:13 before, /device:TPU:6 now
where the time goes in v1:
time: 68 us; the launch traced here: 67.4 us
  Pallas kernels  64 us (94%)
  local copies, waits for them, and re-layouts  2.81 us (4%)
    pallas_call x1, Pallas kernels, body(): pl.pallas_call(functools.partial(kernel, n_ctx, n_head, block, halves), o...  59.7 us
    pallas_call x1, Pallas kernels, body(): pl.pallas_call(project, grid=(width // tile,), out_shape=(jax.ShapeDtypeS...  4.27 us
    unnamed x4, local copies, waits for them, and re-layouts  2.81 us

profile of v1, /device:TPU:6, one launch (start us, length us, event | category | flops | bytes accessed | tf_op | source)
XLA Modules:
  0.0 67.4 jit_solution(13164999655690659971)
XLA Ops:
  0.6 59.7 %path_attention.1 = (bf16[1024,512]{1,0:T(8,128)(2,1)}, bf16[512,2048]{1,0:T(8,128)(2,1)}) custom-call(bf16[1024,128]{1,0:T(8,128)(2,1)} %bitcast.5, bf16[1024,128]{1,0:T(8,128)(2,1)} %bitcast.6, bf16[1024,128]{1,0:T(8,128)(2,1)} %bitcast.7, bf16[1024,128]{1,0:T(8,128)(2,1)} %bitcast.8, f32[1,1024]{1,0:T(1,128)} %rates_ref.1, bf16[128,8192]{1,0:T(8,128)(2,1)} %w_ref.1), custom_call_target="tpu_custom_call" | custom-call | tf_op jit(solution)/shard_map/path_attention/pallas_call | solution.py:375
  60.3 0.0 copy-start
  60.3 1.6 %copy-done = bf16[512,2048]{1,0:T(8,128)(2,1)S(1)} copy-done((bf16[512,2048]{1,0:T(8,128)(2,1)S(1)}, bf16[512,2048]{1,0:T(8,128)(2,1)}, u32[]{:S(2)}) %copy-start) | copy-done | bytes 2097176
  61.9 0.0 copy-start.1
  61.9 1.2 %copy-done.1 = bf16[1024,512]{1,0:T(8,128)(2,1)S(1)} copy-done((bf16[1024,512]{1,0:T(8,128)(2,1)S(1)}, bf16[1024,512]{1,0:T(8,128)(2,1)}, u32[]{:S(2)}) %copy-start.1) | copy-done | bytes 1048600
  63.1 4.3 %projection.1 = (bf16[1024,128]{1,0:T(8,128)(2,1)}, bf16[1024,2048]{1,0:T(8,128)(2,1)}) custom-call(bf16[1024,512]{1,0:T(8,128)(2,1)S(1)} %copy-done.1, bf16[512,2048]{1,0:T(8,128)(2,1)S(1)} %copy-done), custom_call_target="tpu_custom_call" | custom-call | tf_op jit(solution)/shard_map/projection/pallas_call | solution.py:405
Async XLA Ops:
  60.3 1.6 %copy-start = (bf16[512,2048]{1,0:T(8,128)(2,1)S(1)}, bf16[512,2048]{1,0:T(8,128)(2,1)}, u32[]{:S(2)}) copy-start(bf16[512,2048]{1,0:T(8,128)(2,1)} %get-tuple-element.7.cols_ref) | copy-start | bytes 6291460
  61.9 1.2 %copy-start.1 = (bf16[1024,512]{1,0:T(8,128)(2,1)S(1)}, bf16[1024,512]{1,0:T(8,128)(2,1)}, u32[]{:S(2)}) copy-start(bf16[1024,512]{1,0:T(8,128)(2,1)} %get-tuple-element.6.flat_ref) | copy-start | bytes 3145732

commit v2 on v1

v2 whole, which is shorter than its diff:
```python
import functools

import jax
import jax.numpy as jnp
from jax import lax
from jax.experimental import pallas as pl
from jax.experimental.pallas import tpu as pltpu
from jax.sharding import PartitionSpec as P

EPSILON = 1e-06
NEGATIVE = -1e30
MESH = pl.DeviceIdType.MESH
F32 = jnp.float32
BF16 = jnp.bfloat16
NT = (((1,), (1,)), ((), ()))
LOG2E = 1.4426950408889634


def mm(a, b):
    return jnp.dot(a, b, preferred_element_type=F32)


def split(x):
    high = x.astype(BF16)
    return high, (x - high.astype(F32)).astype(BF16)


def twice(x, axis):
    return jnp.concatenate([x, x], axis)


def mm3(a, b):
    (ah, al), (bh, bl) = a, b
    return mm(jnp.concatenate([ah, al], 1), twice(bh, 0)) + mm(ah, bl)


def kernel(
    n_ctx, n_head, block, tile, halves,
    q_hbm, k_hbm, v_hbm, h_hbm, rates_hbm, w_ref,
    attended_ref, proj_ref,
    q_ref, k_ref, v_ref, h_ref, rates_ref, kall, vall, wbuf, flat_ref, att, near, mov, acc, peak,
    v_ssem, v_fsem, v_rsem, v_lsem, k_ssem, k_fsem, k_rsem, k_lsem,
    w_ssem, w_rsem, wf_ssem, wf_rsem, a_ssem, a_rsem, a_fsem, own_sem, in_sem,
):
    me = lax.axis_index("ctx")
    head = lax.axis_index("head")
    rows, feat = q_ref.shape
    blocks = rows // block
    width = wbuf.shape[1]
    half_width = width // 2
    scale = feat ** (-0.5) * LOG2E
    odd = lax.rem(me, 2)
    partner = me + 1 - 2 * odd
    later_pairs = (n_ctx - 1 - me) // 2
    earlier_pairs = me // 2
    span = rows // halves

    loads = [
        pltpu.make_async_copy(source, target, in_sem.at[i]) for i, (source, target) in enumerate((
            (v_hbm, v_ref), (h_hbm, h_ref), (rates_hbm, rates_ref), (k_hbm, k_ref), (q_hbm, q_ref)))]
    for load in loads:
        load.start()

    barrier = pltpu.get_barrier_semaphore()
    for step in range(1, n_ctx):
        pl.semaphore_signal(barrier, inc=1, device_id={"ctx": lax.rem(me + step, n_ctx)}, device_id_type=MESH)
    for step in range(1, n_head):
        pl.semaphore_signal(barrier, inc=1, device_id={"head": lax.rem(head + step, n_head)}, device_id_type=MESH)
    loads[0].wait()
    vall[me, :feat, :] = v_ref[...].T
    pl.semaphore_wait(barrier, n_ctx + n_head - 2)

    def slab(piece, owner, send, recv, peer):
        return pltpu.make_async_remote_copy(
            src_ref=piece, dst_ref=piece, send_sem=send, recv_sem=recv.at[owner],
            device_id={"ctx": peer}, device_id_type=MESH)

    def v_copy(owner, peer):
        return slab(vall.at[owner, :feat], owner, v_ssem.at[peer], v_rsem, peer)

    def k_copy(owner, peer):
        return slab(kall.at[owner], owner, k_ssem.at[peer], k_rsem, peer)

    def v_forward(owner):
        return slab(vall.at[owner, :feat], owner, v_fsem.at[owner], v_rsem, partner)

    def k_forward(owner):
        return slab(kall.at[owner], owner, k_fsem.at[owner], k_rsem, partner)

    def v_relay(owner, peer):
        return slab(vall.at[owner, :feat], owner, v_lsem.at[owner], v_rsem, peer)

    def k_relay(owner, peer):
        return slab(kall.at[owner], owner, k_lsem.at[owner], k_rsem, peer)

    square = n_ctx == 8
    relays = ((2, 0, 6), (5, 1, 7), (7, 3, 5)) if square else ()

    def to_later(copy, action):
        if square:
            @pl.when(me == 2)
            def _():
                action(copy(me, 4))

            for group, targets in ((0, (1, 2)), (1, (3,)), (2, (3,))):
                @pl.when(me // 2 == group)
                def _():
                    for target in targets:
                        action(copy(me, 2 * target + odd))
        else:
            def go(i, carry):
                action(copy(me, me + 2 * (later_pairs - i)))
                return carry
            lax.fori_loop(0, later_pairs, go, 0)

        @pl.when(odd == 0)
        def _():
            action(copy(me, me + 1))

    def half_cols(base, which):
        return pl.ds(pl.multiple_of(base + which * half_width, 128), half_width)

    def w_copy(owner, peer):
        return pltpu.make_async_remote_copy(
            src_ref=w_ref.at[:, half_cols(peer * width, odd)],
            dst_ref=wbuf.at[pl.ds(pl.multiple_of(owner * feat, 128), feat), half_cols(0, odd)],
            send_sem=w_ssem.at[peer], recv_sem=w_rsem.at[owner],
            device_id={"head": peer}, device_id_type=MESH)

    def w_swap(owner, which):
        part = wbuf.at[pl.ds(pl.multiple_of(owner * feat, 128), feat), half_cols(0, which)]
        return pltpu.make_async_remote_copy(
            src_ref=part, dst_ref=part, send_sem=wf_ssem.at[owner], recv_sem=wf_rsem.at[owner],
            device_id={"ctx": partner}, device_id_type=MESH)

    def a_rows(part):
        return pl.ds(part * span, span)

    def a_cols(owner):
        return pl.ds(pl.multiple_of(owner * feat, 128), feat)

    def a_copy(owner, peer, part):
        return pltpu.make_async_remote_copy(
            src_ref=att.at[a_rows(part), :], dst_ref=flat_ref.at[a_rows(part), a_cols(owner)],
            send_sem=a_ssem.at[part, peer], recv_sem=a_rsem.at[part, owner],
            device_id={"head": peer}, device_id_type=MESH)

    def a_relay(owner, peer, part):
        piece = flat_ref.at[a_rows(part), a_cols(owner)]
        return pltpu.make_async_remote_copy(
            src_ref=piece, dst_ref=piece,
            send_sem=a_fsem.at[part, owner], recv_sem=a_rsem.at[part, owner],
            device_id={"head": peer}, device_id_type=MESH)

    for step in range(1, n_head):
        w_copy(head, lax.rem(head + step, n_head)).start()
    w_own = pltpu.make_async_copy(
        w_ref.at[:, pl.ds(pl.multiple_of(head * width, 128), width)],
        wbuf.at[pl.ds(pl.multiple_of(head * feat, 128), feat), :], own_sem.at[0])
    w_own.start()

    ri = lax.broadcasted_iota(jnp.int32, (block, block), 0)
    ci = lax.broadcasted_iota(jnp.int32, (block, block), 1)
    eye = ri == ci
    unit = jnp.where(eye, 1.0, 0.0).astype(F32)
    strict = ri < ci
    every = range(blocks)
    parts = [slice(b * block, (b + 1) * block) for b in every]

    def within(fine, coarse):
        return jnp.logical_and((ri >> coarse) == (ci >> coarse), (ri >> fine) != (ci >> fine))

    for load in loads[1:4]:
        load.wait()
    ups, khs, steps = [], [], []
    for b in every:
        hb, kb = h_ref[parts[b], :], k_ref[parts[b], :]
        both = lax.dot_general(jnp.concatenate([hb, kb], 0), hb, NT, preferred_element_type=F32)
        gram = both[:block]
        norm = jnp.sum(jnp.where(eye, gram, 0.0), axis=0, keepdims=True) + EPSILON
        step_row = rates_ref[:, parts[b]] / norm
        steps.append(jnp.sum(jnp.where(eye, step_row, 0.0), axis=1, keepdims=True))
        ups.append(jnp.where(strict, gram * step_row, 0.0))
        khs.append(jnp.where(strict, both[block:], 0.0))

    to_later(v_copy, lambda copy: copy.start())
    loads[4].wait()
    vall[:, feat:, :] = jnp.ones((n_ctx, vall.shape[1] - feat, rows), BF16)

    base = [jnp.where(within(0, 3), u, 0.0) for u in ups]
    bs = [split(u) for u in base]
    squares = [mm3(p, p) for p in bs]
    qs = [split(x) for x in squares]
    cubes = [mm3(bs[b], qs[b]) for b in every]
    fourths = [mm3(qs[b], qs[b]) for b in every]
    firsts = [unit - base[b] + squares[b] - cubes[b] for b in every]
    invs = [firsts[b] + mm3(split(firsts[b]), split(fourths[b])) for b in every]
    size = 3
    while (1 << size) < block:
        top = min(size + 2, block.bit_length() - 1)
        xs = [split(x) for x in invs]
        offs = [split(jnp.where(within(size, top), u, 0.0)) for u in ups]
        zs = [split(mm3(xs[b], offs[b])) for b in every]
        ones = [invs[b] - mm3(zs[b], xs[b]) for b in every]
        if top == size + 2:
            twos = [split(mm3(zs[b], zs[b])) for b in every]
            ones = [ones[b] + mm3(twos[b], split(ones[b])) for b in every]
        invs = ones
        size = top

    for device, owner, peer in relays:
        @pl.when(me == device)
        def _():
            v_copy(owner, me).wait_recv()
            v_relay(owner, peer).start()

    rights, groups = [], []
    for b in every:
        hb, kb = h_ref[parts[b], :], k_ref[parts[b], :]
        th, tl = split(invs[b] * steps[b])
        kh, kl = split(khs[b])
        left = jnp.concatenate([kh, hb.T], 0)
        right = mm(twice(left, 1), jnp.concatenate([th, tl], 0))
        right = jnp.concatenate([right[:block] + mm(kl, th), right[block:]], 0)
        rh, rl = split(right)
        rights.append((rh, jnp.concatenate([rh, rl], 1)))
        change = mm(rights[b][1], twice(hb, 0))
        groups.append((kb.astype(F32) - change[:block], unit - change[block:]))

    levels = []
    while len(groups) > 1:
        merged, level = [], []
        for g in range(0, len(groups) - 1, 2):
            (early, early_all), (late, late_all) = groups[g], groups[g + 1]
            joined = jnp.concatenate([early, early_all], 0)
            parted = split(joined)
            level.append(parted[0])
            out = mm3(parted, split(late_all))
            merged.append((jnp.concatenate([out[:-feat], late], 0), out[-feat:]))
        levels.append(level)
        groups = merged
    kall[me, :rows, :] = groups[0][0].astype(BF16)
    kall[me, rows:, :] = groups[0][1].astype(BF16)
    to_later(k_copy, lambda copy: copy.start())

    def pass_values(i, carry):
        source = me - 2 - 2 * i
        taken = source < 0
        for device, owner, _ in relays:
            taken = jnp.logical_or(taken, jnp.logical_and(me == device, source == owner))

        @pl.when(jnp.logical_not(taken))
        def _():
            v_copy(source, me).wait_recv()
        v_forward(source).start()
        return carry
    lax.fori_loop(0, earlier_pairs, pass_values, 0)

    moving = []
    for b in every:
        hb, kb, qb = h_ref[parts[b], :], k_ref[parts[b], :], q_ref[parts[b], :]
        both = lax.dot_general(jnp.concatenate([hb, kb], 0), qb, NT, preferred_element_type=F32)
        wh, wl = split(jnp.where(ri <= ci, both[:block], 0.0))
        change = mm(rights[b][1], twice(wh, 0)) + mm(rights[b][0], wl)
        inside = (both[block:] - change[:block]) * scale
        near[parts[b], parts[b]] = jnp.where(ri <= ci, inside, NEGATIVE)
        moving.append((qb.T.astype(F32) - change[block:]) * scale)
    width_now = block
    for level in levels:
        joined = []
        for g, keys in enumerate(level):
            first = 2 * g * width_now
            out = mm(twice(keys, 1), jnp.concatenate(split(moving[2 * g + 1]), 0))
            near[first : first + width_now, first + width_now : first + 2 * width_now] = out[:-feat]
            near[first + width_now : first + 2 * width_now, first : first + width_now] = jnp.full(
                (width_now, width_now), NEGATIVE, F32)
            joined.append(jnp.concatenate([moving[2 * g], out[-feat:]], 1))
        moving = joined
        width_now *= 2
    mov[...] = moving[0]
    for t in range(rows // tile):
        cols = slice(t * tile, (t + 1) * tile)
        seen = (t + 1) * tile
        scores = near[:seen, cols]
        top = jnp.max(scores, axis=0, keepdims=True)
        peak[:, cols] = top
        acc[:, cols] = mm(vall[me, :, :seen], jnp.exp2(scores - top).astype(BF16))

    def attend(tiles, sources):
        every_score = []
        for cols in tiles:
            current = mov[:, cols]
            scores = []
            for source in sources:
                out = mm(twice(kall[source], 1), jnp.concatenate(split(current), 0))
                scores.append(out[:rows])
                current = out[rows:]
            mov[:, cols] = current
            every_score.append(scores)
        for cols, scores in zip(tiles, every_score):
            old = peak[:, cols]
            top = old
            for s in scores:
                top = jnp.maximum(top, jnp.max(s, axis=0, keepdims=True))
            peak[:, cols] = top
            gathered = acc[:, cols] * jnp.exp2(old - top)
            for source, s in zip(sources, scores):
                gathered = gathered + mm(vall[source], jnp.exp2(s - top).astype(BF16))
            acc[:, cols] = gathered

    def relayed(owner, peer):
        if n_head < 3:
            return owner != owner
        return jnp.logical_or(jnp.logical_and(owner == 0, peer == n_head - 1),
                              jnp.logical_and(owner == n_head - 1, peer == 0))

    def direct(part, action):
        for peer in range(n_head):
            @pl.when(jnp.logical_and(head != peer, jnp.logical_not(relayed(head, peer))))
            def _():
                action(a_copy(head, peer, part))

    groups_of = [[pl.ds(part * span + t * tile, tile) for t in range(span // tile)] for part in range(halves)]
    for device, owner, peer in relays:
        @pl.when(me == device)
        def _():
            k_copy(owner, me).wait_recv()
            k_relay(owner, peer).start()
            k_forward(owner).start()

    for part in range(halves):
        @pl.when(odd == 1)
        def _():
            if part == 0:
                k_copy(me - 1, me).wait_recv()
                v_copy(me - 1, me).wait_recv()
            attend(groups_of[part], [me - 1])

        def visit(i, carry):
            low = (earlier_pairs - 1 - i) * 2
            if part == 0:
                mine, other = low + odd, low + 1 - odd
                taken = mine < 0
                for device, owner, _ in relays:
                    taken = jnp.logical_or(taken, jnp.logical_and(me == device, mine == owner))

                @pl.when(jnp.logical_not(taken))
                def _():
                    k_copy(mine, me).wait_recv()
                    k_forward(mine).start()
                k_copy(other, me).wait_recv()
                v_copy(other, me).wait_recv()
            attend(groups_of[part], [low + 1, low])
            return carry

        lax.fori_loop(0, earlier_pairs, visit, 0)
        for cols in groups_of[part]:
            att[cols, :] = (acc[:feat, cols] / acc[feat : feat + 1, cols]).T.astype(BF16)
        direct(part, lambda copy: copy.start())
        attended_ref[a_rows(part), :] = att[a_rows(part), :]
        flat_ref[a_rows(part), a_cols(head)] = att[a_rows(part), :]
        if part == 0:
            for step in range(1, n_head):
                other = lax.rem(head + step, n_head)
                w_copy(other, head).wait_recv()
                w_swap(other, odd).start()
            w_own.wait()

    for step in range(1, n_head):
        w_swap(lax.rem(head + step, n_head), 1 - odd).wait_recv()

    to_later(v_copy, lambda copy: copy.wait_send())
    to_later(k_copy, lambda copy: copy.wait_send())

    def passed(i, carry):
        source = me - 2 - 2 * i
        v_forward(source).wait_send()
        k_forward(source).wait_send()
        return carry
    lax.fori_loop(0, earlier_pairs, passed, 0)
    for device, owner, peer in relays:
        @pl.when(me == device)
        def _():
            v_relay(owner, peer).wait_send()
            k_relay(owner, peer).wait_send()

    for step in range(1, n_head):
        other = lax.rem(head + step, n_head)
        w_copy(head, other).wait_send()
        w_swap(other, odd).wait_send()

    for part in range(halves):
        if n_head >= 3:
            for owner, relay, peer in ((0, n_head - 2, n_head - 1), (n_head - 1, 1, 0)):
                @pl.when(head == relay)
                def _():
                    a_copy(owner, relay, part).wait_recv()
                    a_relay(owner, peer, part).start()
        for owner in range(n_head):
            skip = head != owner
            if n_head >= 3 and owner in (0, n_head - 1):
                skip = jnp.logical_and(skip, head != (n_head - 2 if owner == 0 else 1))

            @pl.when(skip)
            def _():
                a_copy(owner, head, part).wait_recv()

        def project(i, carry):
            out_rows = pl.ds(pl.multiple_of(part * span + (i // strips) * tall, tall), tall)
            out_cols = pl.ds(pl.multiple_of(lax.rem(i, strips) * wide, 128), wide)
            proj_ref[out_rows, out_cols] = mm(flat_ref[out_rows, :], wbuf[:, out_cols]).astype(BF16)
            return carry

        tall, wide = min(256, span), min(512, width)
        strips = width // wide
        lax.fori_loop(0, (span // tall) * strips, project, 0)

    for part in range(halves):
        direct(part, lambda copy: copy.wait_send())
        if n_head >= 3:
            for owner, relay, peer in ((0, n_head - 2, n_head - 1), (n_head - 1, 1, 0)):
                @pl.when(head == relay)
                def _():
                    a_relay(owner, peer, part).wait_send()


def solution(mesh):
    n_ctx, n_head = mesh.shape["ctx"], mesh.shape["head"]

    def body(queries, keys, values, house, rates, out_weight):
        rows, _, feat = queries.shape
        block = feat
        tile = min(256, rows)
        halves = 2 if rows % (2 * tile) == 0 else 1
        width = out_weight.shape[1] // n_head
        vmem = pl.BlockSpec(memory_space=pltpu.VMEM)
        hbm = pl.BlockSpec(memory_space=pltpu.HBM)
        dma = pltpu.SemaphoreType.DMA
        attended, projected = pl.pallas_call(
            functools.partial(kernel, n_ctx, n_head, block, tile, halves),
            out_shape=(
                pltpu.VMEM((rows, feat), BF16),
                pltpu.VMEM((rows, width), BF16),
            ),
            in_specs=[hbm] * 6,
            out_specs=(vmem, vmem),
            scratch_shapes=[pltpu.VMEM((rows, feat), BF16)] * 4 + [
                pltpu.VMEM((1, rows), F32),
                pltpu.VMEM((n_ctx, rows + feat, feat), BF16),
                pltpu.VMEM((n_ctx, feat + 16, rows), BF16),
                pltpu.VMEM((n_head * feat, width), BF16),
                pltpu.VMEM((rows, n_head * feat), BF16),
                pltpu.VMEM((rows, feat), BF16),
                pltpu.VMEM((rows, rows), F32),
                pltpu.VMEM((feat, rows), F32),
                pltpu.VMEM((feat + 16, rows), F32),
                pltpu.VMEM((1, rows), F32),
                dma((n_ctx,)), dma((n_ctx,)), dma((n_ctx,)), dma((n_ctx,)), dma((n_ctx,)), dma((n_ctx,)), dma((n_ctx,)), dma((n_ctx,)),
                dma((n_head,)), dma((n_head,)), dma((n_head,)), dma((n_head,)),
                dma((halves, n_head)), dma((halves, n_head)), dma((halves, n_head)), dma((1,)), dma((5,)),
            ],
            compiler_params=pltpu.CompilerParams(
                collective_id=0, has_side_effects=True, vmem_limit_bytes=66 * 1000 * 1000 - 2 * rows * (width + feat)),
            name="path_attention",
        )(queries.reshape(rows, feat), keys.reshape(rows, feat), values.reshape(rows, feat),
          house.reshape(rows, feat), rates, out_weight)
        return attended.reshape(rows, 1, feat), projected

    in_specs = (
        P("ctx", "head", None),
        P("ctx", "head", None),
        P("ctx", "head", None),
        P("ctx", "head", None),
        P("head", "ctx"),
        P("head", None),
    )
    out_specs = (P("ctx", "head", None), P("ctx", "head"))
    return jax.shard_map(body, mesh=mesh, in_specs=in_specs, out_specs=out_specs, check_vma=False)
```

time: 68 us -> 58.9 us (0.87)
  Pallas kernels: 64 us -> 55.1 us
    pallas_call x2 -> x1, Pallas kernels: 64 us -> 55.1 us  [body(): pl.pallas_call(functools.partial(kernel, n_ctx, n_head, block, tile, halv...]
    unnamed x4 -> x2, local copies, waits for them, and re-layouts: 2.81 us -> 2.72 us
where the time goes in v2:
time: 58.9 us; the launch traced here: 58.5 us
  Pallas kernels  55.1 us (94%)
  local copies, waits for them, and re-layouts  2.72 us (5%)
  between operations  0.64 us (1%)
    pallas_call x1, Pallas kernels, body(): pl.pallas_call(functools.partial(kernel, n_ctx, n_head, block, tile, halv...  55.1 us
    unnamed x2, local copies, waits for them, and re-layouts  2.72 us

profile of v2, /device:TPU:6, one launch (start us, length us, event | category | flops | bytes accessed | tf_op | source)
XLA Modules:
  0.0 58.5 jit_solution(1770957690960681784)
XLA Ops:
  0.6 55.1 %path_attention.1 = (bf16[1024,128]{1,0:T(8,128)(2,1)S(1)}, bf16[1024,2048]{1,0:T(8,128)(2,1)S(1)}) custom-call(bf16[1024,128]{1,0:T(8,128)(2,1)} %bitcast.6, bf16[1024,128]{1,0:T(8,128)(2,1)} %bitcast.7, bf16[1024,128]{1,0:T(8,128)(2,1)} %bitcast.8, bf16[1024,128]{1,0:T(8,128)(2,1)} %bitcast.9, f32[1,1024]{1,0:T(1,128)} %rates_hbm.1, bf16[128,8192]{1,0:T(8,128)(2,1)} %w_ref.1), custom_call_target="tpu_custom_call" | custom-call | tf_op jit(solution)/shard_map/path_attention/pallas_call | solution.py:439
  55.7 0.7 %copy.10 = bf16[1024,1,128]{2,0,1:T(8,128)(2,1)} copy(bf16[1024,1,128]{2,0,1:T(8,128)(2,1)S(1)} %bitcast.5) | data formatting | bytes 524288
  56.5 2.0 %copy.11 = bf16[1024,2048]{1,0:T(8,128)(2,1)} copy(bf16[1024,2048]{1,0:T(8,128)(2,1)S(1)} %get-tuple-element.7) | data formatting | bytes 8388608

commit v3 on v2

--- a/solution.py
+++ b/solution.py
@@ -47,7 +47,10 @@
     rows, feat = q_ref.shape
     blocks = rows // block
     width = wbuf.shape[1]
-    half_width = width // 2
+    share = 4 if n_ctx % 4 == 0 else 2
+    quarter = width // share
+    mine_q = lax.rem(me, share)
+    across = me + 2 - 4 * (lax.rem(me, 4) // 2)
     scale = feat ** (-0.5) * LOG2E
     odd = lax.rem(me, 2)
     partner = me + 1 - 2 * odd
@@ -94,13 +97,15 @@
         return slab(kall.at[owner], owner, k_lsem.at[owner], k_rsem, peer)
 
     square = n_ctx == 8
-    relays = ((2, 0, 6), (5, 1, 7), (7, 3, 5)) if square else ()
-
-    def to_later(copy, action):
+    v_relays = ((2, 0, 6), (5, 1, 7), (6, 2, 4), (7, 3, 5)) if square else ()
+    k_relays = ((2, 0, 6), (5, 1, 7), (7, 3, 5)) if square else ()
+
+    def to_later(copy, action, whole=True):
         if square:
-            @pl.when(me == 2)
-            def _():
-                action(copy(me, 4))
+            if not whole:
+                @pl.when(me == 2)
+                def _():
+                    action(copy(me, 4))
 
             for group, targets in ((0, (1, 2)), (1, (3,)), (2, (3,))):
                 @pl.when(me // 2 == group)
@@ -117,21 +122,27 @@
         def _():
             action(copy(me, me + 1))
 
-    def half_cols(base, which):
-        return pl.ds(pl.multiple_of(base + which * half_width, 128), half_width)
+    def quarter_cols(base, which):
+        return pl.ds(pl.multiple_of(base + which * quarter, 128), quarter)
+
+    def w_piece(owner, which):
+        return wbuf.at[pl.ds(pl.multiple_of(owner * feat, 128), feat), quarter_cols(0, which)]
 
     def w_copy(owner, peer):
         return pltpu.make_async_remote_copy(
-            src_ref=w_ref.at[:, half_cols(peer * width, odd)],
-            dst_ref=wbuf.at[pl.ds(pl.multiple_of(owner * feat, 128), feat), half_cols(0, odd)],
+            src_ref=w_ref.at[:, quarter_cols(peer * width, mine_q)], dst_ref=w_piece(owner, mine_q),
             send_sem=w_ssem.at[peer], recv_sem=w_rsem.at[owner],
             device_id={"head": peer}, device_id_type=MESH)
 
-    def w_swap(owner, which):
-        part = wbuf.at[pl.ds(pl.multiple_of(owner * feat, 128), feat), half_cols(0, which)]
+    def w_hand(owner, which, way, peer):
         return pltpu.make_async_remote_copy(
-            src_ref=part, dst_ref=part, send_sem=wf_ssem.at[owner], recv_sem=wf_rsem.at[owner],
-            device_id={"ctx": partner}, device_id_type=MESH)
+            src_ref=w_piece(owner, which), dst_ref=w_piece(owner, which),
+            send_sem=wf_ssem.at[way, owner], recv_sem=wf_rsem.at[way, owner],
+            device_id={"ctx": peer}, device_id_type=MESH)
+
+    beside = mine_q + 1 - 2 * odd
+    over = lax.rem(mine_q + 2, share)
+    over_beside = lax.rem(beside + 2, share)
 
     def a_rows(part):
         return pl.ds(part * span, span)
@@ -183,7 +194,7 @@
         ups.append(jnp.where(strict, gram * step_row, 0.0))
         khs.append(jnp.where(strict, both[block:], 0.0))
 
-    to_later(v_copy, lambda copy: copy.start())
+    to_later(v_copy, lambda copy: copy.start(), True)
     loads[4].wait()
     vall[:, feat:, :] = jnp.ones((n_ctx, vall.shape[1] - feat, rows), BF16)
 
@@ -208,7 +219,7 @@
         invs = ones
         size = top
 
-    for device, owner, peer in relays:
+    for device, owner, peer in v_relays:
         @pl.when(me == device)
         def _():
             v_copy(owner, me).wait_recv()
@@ -241,20 +252,7 @@
         groups = merged
     kall[me, :rows, :] = groups[0][0].astype(BF16)
     kall[me, rows:, :] = groups[0][1].astype(BF16)
-    to_later(k_copy, lambda copy: copy.start())
-
-    def pass_values(i, carry):
-        source = me - 2 - 2 * i
-        taken = source < 0
-        for device, owner, _ in relays:
-            taken = jnp.logical_or(taken, jnp.logical_and(me == device, source == owner))
-
-        @pl.when(jnp.logical_not(taken))
-        def _():
-            v_copy(source, me).wait_recv()
-        v_forward(source).start()
-        return carry
-    lax.fori_loop(0, earlier_pairs, pass_values, 0)
+    to_later(k_copy, lambda copy: copy.start(), False)
 
     moving = []
     for b in every:
@@ -308,6 +306,19 @@
                 gathered = gathered + mm(vall[source], jnp.exp2(s - top).astype(BF16))
             acc[:, cols] = gathered
 
+    def pass_values(i, carry):
+        source = me - 2 - 2 * i
+        taken = source < 0
+        for device, owner, _ in v_relays:
+            taken = jnp.logical_or(taken, jnp.logical_and(me == device, source == owner))
+
+        @pl.when(jnp.logical_not(taken))
+        def _():
+            v_copy(source, me).wait_recv()
+        v_forward(source).start()
+        return carry
+    lax.fori_loop(0, earlier_pairs, pass_values, 0)
+
     def relayed(owner, peer):
         if n_head < 3:
             return owner != owner
@@ -315,13 +326,16 @@
                               jnp.logical_and(owner == n_head - 1, peer == 0))
 
     def direct(part, action):
-        for peer in range(n_head):
-            @pl.when(jnp.logical_and(head != peer, jnp.logical_not(relayed(head, peer))))
-            def _():
-                action(a_copy(head, peer, part))
+        for beyond, peers in ((True, range(n_head - 1, 0, -1)), (False, range(n_head - 1))):
+            for peer in peers:
+                wanted = head < peer if beyond else head > peer
+
+                @pl.when(jnp.logical_and(wanted, jnp.logical_not(relayed(head, peer))))
+                def _():
+                    action(a_copy(head, peer, part))
 
     groups_of = [[pl.ds(part * span + t * tile, tile) for t in range(span // tile)] for part in range(halves)]
-    for device, owner, peer in relays:
+    for device, owner, peer in k_relays:
         @pl.when(me == device)
         def _():
             k_copy(owner, me).wait_recv()
@@ -341,7 +355,7 @@
             if part == 0:
                 mine, other = low + odd, low + 1 - odd
                 taken = mine < 0
-                for device, owner, _ in relays:
+                for device, owner, _ in k_relays:
                     taken = jnp.logical_or(taken, jnp.logical_and(me == device, mine == owner))
 
                 @pl.when(jnp.logical_not(taken))
@@ -363,14 +377,23 @@
             for step in range(1, n_head):
                 other = lax.rem(head + step, n_head)
                 w_copy(other, head).wait_recv()
-                w_swap(other, odd).start()
+                w_hand(other, mine_q, 0, partner).start()
+                if share == 4:
+                    w_hand(other, mine_q, 1, across).start()
             w_own.wait()
 
-    for step in range(1, n_head):
-        w_swap(lax.rem(head + step, n_head), 1 - odd).wait_recv()
-
-    to_later(v_copy, lambda copy: copy.wait_send())
-    to_later(k_copy, lambda copy: copy.wait_send())
+    others = [lax.rem(head + step, n_head) for step in range(1, n_head)]
+    if share == 4:
+        for other in others:
+            w_hand(other, over, 1, across).wait_recv()
+            w_hand(other, over, 2, partner).start()
+        for other in others:
+            w_hand(other, over_beside, 2, partner).wait_recv()
+    for other in others:
+        w_hand(other, beside, 0, partner).wait_recv()
+
+    to_later(v_copy, lambda copy: copy.wait_send(), True)
+    to_later(k_copy, lambda copy: copy.wait_send(), False)
 
     def passed(i, carry):
         source = me - 2 - 2 * i
@@ -378,16 +401,19 @@
         k_forward(source).wait_send()
         return carry
     lax.fori_loop(0, earlier_pairs, passed, 0)
-    for device, owner, peer in relays:
-        @pl.when(me == device)
-        def _():
-            v_relay(owner, peer).wait_send()
-            k_relay(owner, peer).wait_send()
+    for relays, relay_copy in ((v_relays, v_relay), (k_relays, k_relay)):
+        for device, owner, peer in relays:
+            @pl.when(me == device)
+            def _():
+                relay_copy(owner, peer).wait_send()
 
     for step in range(1, n_head):
         other = lax.rem(head + step, n_head)
         w_copy(head, other).wait_send()
-        w_swap(other, odd).wait_send()
+        w_hand(other, mine_q, 0, partner).wait_send()
+        if share == 4:
+            w_hand(other, mine_q, 1, across).wait_send()
+            w_hand(other, over, 2, partner).wait_send()
 
     for part in range(halves):
         if n_head >= 3:
@@ -456,7 +482,7 @@
                 pltpu.VMEM((feat + 16, rows), F32),
                 pltpu.VMEM((1, rows), F32),
                 dma((n_ctx,)), dma((n_ctx,)), dma((n_ctx,)), dma((n_ctx,)), dma((n_ctx,)), dma((n_ctx,)), dma((n_ctx,)), dma((n_ctx,)),
-                dma((n_head,)), dma((n_head,)), dma((n_head,)), dma((n_head,)),
+                dma((n_head,)), dma((n_head,)), dma((3, n_head)), dma((3, n_head)),
                 dma((halves, n_head)), dma((halves, n_head)), dma((halves, n_head)), dma((1,)), dma((5,)),
             ],
             compiler_params=pltpu.CompilerParams(

time: 58.9 us -> 57.5 us (0.976)
  Pallas kernels: 55.1 us -> 54 us
    pallas_call x1, Pallas kernels: 55.1 us -> 54 us  [body(): pl.pallas_call(functools.partial(kernel, n_ctx, n_head, block, tile, halv...]
where the time goes in v3:
time: 57.5 us; the launch traced here: 57.4 us
  Pallas kernels  54 us (94%)
  local copies, waits for them, and re-layouts  2.72 us (5%)
  between operations  0.64 us (1%)
    pallas_call x1, Pallas kernels, body(): pl.pallas_call(functools.partial(kernel, n_ctx, n_head, block, tile, halv...  54 us
    unnamed x2, local copies, waits for them, and re-layouts  2.72 us

profile of v3, /device:TPU:6, one launch (start us, length us, event | category | flops | bytes accessed | tf_op | source)
XLA Modules:
  0.0 57.4 jit_solution(11936674165822436179)
XLA Ops:
  0.6 54.0 %path_attention.1 = (bf16[1024,128]{1,0:T(8,128)(2,1)S(1)}, bf16[1024,2048]{1,0:T(8,128)(2,1)S(1)}) custom-call(bf16[1024,128]{1,0:T(8,128)(2,1)} %bitcast.6, bf16[1024,128]{1,0:T(8,128)(2,1)} %bitcast.7, bf16[1024,128]{1,0:T(8,128)(2,1)} %bitcast.8, bf16[1024,128]{1,0:T(8,128)(2,1)} %bitcast.9, f32[1,1024]{1,0:T(1,128)} %rates_hbm.1, bf16[128,8192]{1,0:T(8,128)(2,1)} %w_ref.1), custom_call_target="tpu_custom_call" | custom-call | tf_op jit(solution)/shard_map/path_attention/pallas_call | solution.py:465
  54.6 0.7 %copy.10 = bf16[1024,1,128]{2,0,1:T(8,128)(2,1)} copy(bf16[1024,1,128]{2,0,1:T(8,128)(2,1)S(1)} %bitcast.5) | data formatting | bytes 524288
  55.3 2.0 %copy.11 = bf16[1024,2048]{1,0:T(8,128)(2,1)} copy(bf16[1024,2048]{1,0:T(8,128)(2,1)S(1)} %get-tuple-element.7) | data formatting | bytes 8388608

commit v4 on v3

--- a/solution.py
+++ b/solution.py
@@ -57,6 +57,8 @@
     later_pairs = (n_ctx - 1 - me) // 2
     earlier_pairs = me // 2
     span = rows // halves
+    pieces = 2 * halves
+    strip = rows // pieces
 
     loads = [
         pltpu.make_async_copy(source, target, in_sem.at[i]) for i, (source, target) in enumerate((
@@ -145,7 +147,7 @@
     over_beside = lax.rem(beside + 2, share)
 
     def a_rows(part):
-        return pl.ds(part * span, span)
+        return pl.ds(part * strip, strip)
 
     def a_cols(owner):
         return pl.ds(pl.multiple_of(owner * feat, 128), feat)
@@ -370,9 +372,11 @@
         lax.fori_loop(0, earlier_pairs, visit, 0)
         for cols in groups_of[part]:
             att[cols, :] = (acc[:feat, cols] / acc[feat : feat + 1, cols]).T.astype(BF16)
-        direct(part, lambda copy: copy.start())
-        attended_ref[a_rows(part), :] = att[a_rows(part), :]
-        flat_ref[a_rows(part), a_cols(head)] = att[a_rows(part), :]
+        for piece in (2 * part, 2 * part + 1):
+            direct(piece, lambda copy: copy.start())
+        held = pl.ds(part * span, span)
+        attended_ref[held, :] = att[held, :]
+        flat_ref[held, a_cols(head)] = att[held, :]
         if part == 0:
             for step in range(1, n_head):
                 other = lax.rem(head + step, n_head)
@@ -415,7 +419,7 @@
             w_hand(other, mine_q, 1, across).wait_send()
             w_hand(other, over, 2, partner).wait_send()
 
-    for part in range(halves):
+    for part in range(pieces):
         if n_head >= 3:
             for owner, relay, peer in ((0, n_head - 2, n_head - 1), (n_head - 1, 1, 0)):
                 @pl.when(head == relay)
@@ -432,16 +436,16 @@
                 a_copy(owner, head, part).wait_recv()
 
         def project(i, carry):
-            out_rows = pl.ds(pl.multiple_of(part * span + (i // strips) * tall, tall), tall)
+            out_rows = pl.ds(pl.multiple_of(part * strip + (i // strips) * tall, tall), tall)
             out_cols = pl.ds(pl.multiple_of(lax.rem(i, strips) * wide, 128), wide)
             proj_ref[out_rows, out_cols] = mm(flat_ref[out_rows, :], wbuf[:, out_cols]).astype(BF16)
             return carry
 
-        tall, wide = min(256, span), min(512, width)
+        tall, wide = min(256, strip), min(512, width)
         strips = width // wide
-        lax.fori_loop(0, (span // tall) * strips, project, 0)
-
-    for part in range(halves):
+        lax.fori_loop(0, (strip // tall) * strips, project, 0)
+
+    for part in range(pieces):
         direct(part, lambda copy: copy.wait_send())
         if n_head >= 3:
             for owner, relay, peer in ((0, n_head - 2, n_head - 1), (n_head - 1, 1, 0)):
@@ -483,7 +487,7 @@
                 pltpu.VMEM((1, rows), F32),
                 dma((n_ctx,)), dma((n_ctx,)), dma((n_ctx,)), dma((n_ctx,)), dma((n_ctx,)), dma((n_ctx,)), dma((n_ctx,)), dma((n_ctx,)),
                 dma((n_head,)), dma((n_head,)), dma((3, n_head)), dma((3, n_head)),
-                dma((halves, n_head)), dma((halves, n_head)), dma((halves, n_head)), dma((1,)), dma((5,)),
+                dma((2 * halves, n_head)), dma((2 * halves, n_head)), dma((2 * halves, n_head)), dma((1,)), dma((5,)),
             ],
             compiler_params=pltpu.CompilerParams(
                 collective_id=0, has_side_effects=True, vmem_limit_bytes=66 * 1000 * 1000 - 2 * rows * (width + feat)),

time: 57.5 us -> 57.2 us (level)
  Pallas kernels: 54 us -> 53.2 us
    pallas_call x1, Pallas kernels: 54 us -> 53.2 us  [body(): pl.pallas_call(functools.partial(kernel, n_ctx, n_head, block, tile, halv...]
where the time goes in v4:
time: 57.2 us; the launch traced here: 56.6 us
  Pallas kernels  53.2 us (93%)
  local copies, waits for them, and re-layouts  2.72 us (5%)
  between operations  0.64 us (1%)
    pallas_call x1, Pallas kernels, body(): pl.pallas_call(functools.partial(kernel, n_ctx, n_head, block, tile, halv...  53.2 us
    unnamed x2, local copies, waits for them, and re-layouts  2.72 us

profile of v4, /device:TPU:6, one launch (start us, length us, event | category | flops | bytes accessed | tf_op | source)
XLA Modules:
  0.0 56.6 jit_solution(9745045011375487633)
XLA Ops:
  0.6 53.2 %path_attention.1 = (bf16[1024,128]{1,0:T(8,128)(2,1)S(1)}, bf16[1024,2048]{1,0:T(8,128)(2,1)S(1)}) custom-call(bf16[1024,128]{1,0:T(8,128)(2,1)} %bitcast.6, bf16[1024,128]{1,0:T(8,128)(2,1)} %bitcast.7, bf16[1024,128]{1,0:T(8,128)(2,1)} %bitcast.8, bf16[1024,128]{1,0:T(8,128)(2,1)} %bitcast.9, f32[1,1024]{1,0:T(1,128)} %rates_hbm.1, bf16[128,8192]{1,0:T(8,128)(2,1)} %w_ref.1), custom_call_target="tpu_custom_call" | custom-call | tf_op jit(solution)/shard_map/path_attention/pallas_call | solution.py:469
  53.8 0.7 %copy.10 = bf16[1024,1,128]{2,0,1:T(8,128)(2,1)} copy(bf16[1024,1,128]{2,0,1:T(8,128)(2,1)S(1)} %bitcast.5) | data formatting | bytes 524288
  54.6 2.0 %copy.11 = bf16[1024,2048]{1,0:T(8,128)(2,1)} copy(bf16[1024,2048]{1,0:T(8,128)(2,1)S(1)} %get-tuple-element.7) | data formatting | bytes 8388608
